TPU v7x, 512 devices: a whole 4x4x16 slice. The times are simulated.
512 devices in a mesh: orb: 64 (over z, y), fft: 8 (over x, core).
Axes of the slice: x: 4, y: 4, z: 16, core: 2. Of those that a mesh axis runs over, the one named last changes fastest.
Arguments:
- orbitals: bfloat16 [512, 256, 256], P('orb', 'fft'), may hold values from -6 to 6
- kernel: float32 [256, 256], P('fft'), may hold values from 0.02 to 2
- partner_owner: int32 [512, 2, 1], P('orb'), may hold values from 0 to 63; in each aligned block of 16 rows (0 to 15, 16 to 31, ..., all dimensions but the last counted through in order) at most 2 rows name the same one
- partner_local: int32 [512, 2], P('orb'), may hold values from 0 to 7
Outputs:
- exchange_term: float32 [512, 256, 256], P('orb', 'fft')
Inputs may be any that keep to these rules, and one draw needn't show every extreme that they name: `partner_owner`: among the 16 partners named on one index of orb, no owner is named more than 2 times, a bound that some block reaches; every owner is named somewhere.
All inputs are finite; a program needn't handle non-finite values.
Results may differ from a plain program's by a relative error of at most 0.0004.
Values may be sent and summed in bfloat16 or wider, within the bound.
No kernel may reach another device: no remote copies, remote signals or barrier semaphores. Data moves between devices by JAX's collectives and lax.ppermute only.
A program may use at most 64 MiB of HBM per device.

v0:
```python
import math
import jax
import jax.numpy as jnp
from jax import lax
from jax.sharding import PartitionSpec as P


def sent_to_all(x, axis):
    count = lax.axis_size(axis)
    return lax.all_to_all(jnp.broadcast_to(x[None], (count, *x.shape)), axis, 0, 0, tiled=True)


def in_order(tiles, dim):
    tiles = jnp.moveaxis(tiles, 0, dim)
    shape = tiles.shape
    return tiles.reshape(*shape[:dim], shape[dim] * shape[dim + 1], *shape[dim + 2 :])


def gathered_copies(x, axis, dim):
    tiles = sent_to_all(x, axis)
    return in_order(tiles, dim)


def tables(length):
    series = jnp.arange(length, dtype=jnp.int32)
    phase = series[:, None] * series[None, :] % length
    angle = phase.astype(jnp.float32) * (2.0 * math.pi / length)
    return (jnp.cos(angle), jnp.sin(angle))


def product(form, left, right):
    return jnp.einsum(form, left, right, precision=lax.Precision.HIGHEST)


def group_potential(density, kernel):
    grouped = lax.all_to_all(density, "fft", split_axis=0, concat_axis=1, tiled=True)
    whole = gathered_copies(kernel, "fft", 0)
    full_x = grouped.shape[1]
    width_y = grouped.shape[2]
    cos_y, sin_y = tables(width_y)
    cos_x, sin_x = tables(full_x)
    real_y = product("txy,yk->txk", grouped, cos_y)
    imag_y = -product("txy,yk->txk", grouped, sin_y)
    f_real = product("txk,xq->tqk", real_y, cos_x) + product("txk,xq->tqk", imag_y, sin_x)
    f_imag = product("txk,xq->tqk", imag_y, cos_x) - product("txk,xq->tqk", real_y, sin_x)
    weight = whole.T
    g_real = weight[None] * f_real
    g_imag = weight[None] * f_imag
    h_real = product("tqk,qx->txk", g_real, cos_x) - product("tqk,qx->txk", g_imag, sin_x)
    h_imag = product("tqk,qx->txk", g_real, sin_x) + product("tqk,qx->txk", g_imag, cos_x)
    spread = product("txk,ky->txy", h_real, cos_y) - product("txk,ky->txy", h_imag, sin_y)
    spread = spread / (full_x * width_y)
    return lax.all_to_all(spread, "fft", split_axis=1, concat_axis=0, tiled=True)


def on_device(orbitals, kernel, partner_owner, partner_local):
    peer_count = lax.axis_size("orb")
    orb_dev, rows_x, width_y = orbitals.shape
    task_count = partner_local.shape[0]
    wanted_count = 2 * task_count
    capacity = max(2, (4 * task_count + peer_count - 1) // peer_count)
    owner_ids = partner_owner.reshape(wanted_count)
    local_ids = partner_local.reshape(wanted_count)
    peer_ids = jnp.arange(peer_count, dtype=jnp.int32)
    owner_hot = (owner_ids[:, None] == peer_ids[None, :]).astype(jnp.int32)
    earlier = jnp.cumsum(owner_hot, axis=0) - owner_hot
    position = jnp.sum(earlier * owner_hot, axis=1)
    target = owner_ids * capacity + position
    slot_ids = jnp.arange(peer_count * capacity, dtype=jnp.int32)
    placed = target[:, None] == slot_ids[None, :]
    wanted = jnp.max(jnp.where(placed, local_ids[:, None], -1), axis=0).reshape(
        peer_count, capacity
    )
    asked = lax.all_to_all(wanted, "orb", split_axis=0, concat_axis=0, tiled=True)
    flat_asked = asked.reshape(peer_count * capacity)
    present = flat_asked >= 0
    picked = jnp.take(orbitals, jnp.clip(flat_asked, 0, orb_dev - 1), axis=0)
    served = jnp.where(present[:, None, None], picked, jnp.zeros_like(picked))
    served = served.reshape(peer_count, capacity, rows_x, width_y)
    arrived = lax.all_to_all(served, "orb", split_axis=0, concat_axis=0, tiled=True)
    arrived = arrived.reshape(peer_count * capacity, rows_x, width_y)
    chosen = (
        jnp.take(arrived, target, axis=0)
        .reshape(task_count, 2, rows_x, width_y)
        .astype(jnp.float32)
    )
    left_orbital = chosen[:, 0]
    right_orbital = chosen[:, 1]
    density = left_orbital * right_orbital
    potential = group_potential(density, kernel)
    contrib = jnp.stack([potential * right_orbital, potential * left_orbital], axis=1)
    contrib = contrib.reshape(wanted_count, rows_x, width_y)
    outgoing = (
        jnp.zeros((peer_count * capacity, rows_x, width_y), jnp.float32).at[target].set(contrib)
    )
    outgoing = outgoing.reshape(peer_count, capacity, rows_x, width_y)
    incoming = lax.all_to_all(outgoing, "orb", split_axis=0, concat_axis=0, tiled=True)
    incoming = incoming.reshape(peer_count * capacity, rows_x * width_y)
    select = (flat_asked[None, :] == jnp.arange(orb_dev, dtype=jnp.int32)[:, None]).astype(
        jnp.float32
    )
    total = jnp.dot(select, incoming, precision=lax.Precision.HIGHEST)
    return (-total).reshape(orb_dev, rows_x, width_y)


def solution(mesh):
    in_specs = (P("orb", "fft", None), P("fft", None), P("orb", None, None), P("orb", None))
    out_specs = P("orb", "fft", None)
    return jax.shard_map(
        on_device, mesh=mesh, in_specs=in_specs, out_specs=out_specs, check_vma=False
    )
```

profile of v0, /device:TPU:8, one launch (start us, length us, event | category | flops | bytes accessed | tf_op | source)
XLA Modules:
  0.0 404.2 jit_solution(12548411028635859213)
XLA Ops:
  0.0 0.0 copy-start
  0.0 0.8 copy.55
  0.8 0.1 broadcast_in_dim.66
  0.9 0.8 copy.54
  1.6 0.1 reshape.189
  1.7 0.1 fusion.30
  1.8 0.2 select_reduce_fusion.1
  2.0 0.1 select_reduce_fusion
  2.1 0.1 all_to_all.31
  2.3 32.3 %all_to_all.45 = s32[64,1,2]{2,1,0:T(1,128)S(1)} all-to-all(s32[64,1,2]{2,1,0:T(1,128)S(1)} %bitcast.64), channel_id=1, replica_groups=mesh['orb'=64,'fft'=8] {'orb'}, dimensions={0} | all-to-all | bytes 1024 | tf_op jit(solution)/shard_map/all_to_all | solution.py:74
  34.6 0.1 copy.61
  34.7 0.1 copy.62
  34.8 0.1 copy.64
  34.9 0.1 copy.65
  35.0 0.1 min.18
  35.2 0.0 copy-done
  35.2 0.7 gather_fusion
  35.9 1.6 select_select_fusion
  37.5 0.0 copy-start.2
  37.5 0.0 copy-start.1
  37.5 5.5 %all-to-all-start.2 = ((bf16[64,2,32,256]{3,2,1,0:T(8,128)(2,1)}), bf16[64,2,32,256]{3,2,1,0:T(8,128)(2,1)S(1)}, u32[]{:S(2)}, u32[]{:S(2)}) async-start(bf16[64,2,32,256]{3,2,1,0:T(8,128)(2,1)} %select_select_fusion), calls=%async_computation.2 | async-start | bytes 4194304 | tf_op jit(solution)/shard_map/all_to_all | solution.py:80
  43.0 0.1 reduce_sum.15
  43.1 0.0 copy-done.2
  43.1 0.1 copy.57
  43.2 0.1 mul.164
  43.3 0.1 copy.59
  43.4 0.1 copy.60
  43.5 98.6 %all-to-all-done.2 = bf16[64,2,32,256]{3,2,1,0:T(8,128)(2,1)S(1)} async-done(((bf16[64,2,32,256]{3,2,1,0:T(8,128)(2,1)}), bf16[64,2,32,256]{3,2,1,0:T(8,128)(2,1)S(1)}, u32[]{:S(2)}, u32[]{:S(2)}) %all-to-all-start.2) | async-done | bytes 2097184 | tf_op jit(solution)/shard_map/all_to_all | solution.py:80
  142.1 0.0 copy-done.1
  142.1 0.7 broadcast_in_dim.70
  142.8 4.3 %all-to-all-start.1 = ((f32[8,32,256]{2,1,0:T(8,128)}), f32[8,32,256]{2,1,0:T(8,128)S(1)}, u32[]{:S(2)}, u32[]{:S(2)}) async-start(f32[8,32,256]{2,1,0:T(8,128)} %broadcast_in_dim.70), calls=%async_computation.1 | async-start | bytes 524288 | tf_op jit(solution)/shard_map/all_to_all | solution.py:10
  147.1 0.6 gather_fusion.1
  147.7 0.1 select_convert_fusion
  147.8 0.7 multiply_bitcast_fusion
  148.6 6.1 %all-to-all-done.1 = f32[8,32,256]{2,1,0:T(8,128)S(1)} async-done(((f32[8,32,256]{2,1,0:T(8,128)}), f32[8,32,256]{2,1,0:T(8,128)S(1)}, u32[]{:S(2)}, u32[]{:S(2)}) %all-to-all-start.1) | async-done | bytes 262176 | tf_op jit(solution)/shard_map/all_to_all | solution.py:10
  154.6 3.6 all-to-all-start.3
  158.2 0.1 copy.58
  158.4 7.1 %all-to-all-done.3 = f32[8,32,256]{2,1,0:T(8,128)S(1)} async-done(((f32[8,32,256]{2,1,0:T(8,128)}), f32[8,32,256]{2,1,0:T(8,128)S(1)}, u32[]{:S(2)}, u32[]{:S(2)}) %all-to-all-start.3) | async-done | bytes 262176 | tf_op jit(solution)/shard_map/all_to_all | solution.py:36
  165.5 1.4 convolution_negate_fusion.1
  166.9 1.3 fusion.21
  168.2 1.8 fusion.19
  170.0 1.8 fusion.15
  171.8 1.8 fusion.3
  173.5 1.8 fusion.24
  175.3 1.8 fusion.17
  177.1 1.8 fusion.2
  178.9 1.8 convolution_subtract_fusion.1
  180.6 2.0 convolution_add_fusion
  182.6 1.3 fusion.13
  184.0 1.4 fusion.1
  185.4 0.3 copy.66
  185.6 9.9 %all_to_all.46 = f32[1,256,256]{2,0,1:T(1,128)S(1)} all-to-all(f32[1,256,256]{2,0,1:T(1,128)S(1)} %copy.66), channel_id=1, replica_groups=mesh['orb'=64,'fft'=8] {'fft'}, dimensions={1} | all-to-all | bytes 524288 | tf_op jit(solution)/shard_map/all_to_all | solution.py:53
  195.6 0.1 slice_multiply_fusion
  195.7 2.5 broadcast_in_dim.69
  198.2 2.6 scatter_fusion
  200.8 6.1 %all-to-all-start.5 = ((f32[64,2,32,256]{3,2,1,0:T(8,128)}), f32[64,2,32,256]{3,2,1,0:T(8,128)}, u32[]{:S(2)}, u32[]{:S(2)}) async-start(f32[64,2,32,256]{3,2,1,0:T(8,128)} %bitcast.53), calls=%async_computation.5 | async-start | bytes 8388608 | tf_op jit(solution)/shard_map/all_to_all | solution.py:97
  206.9 0.5 broadcast.212
  207.4 0.7 reduce.3
  208.1 0.1 eq.50
  208.3 188.2 %all-to-all-done.5 = f32[64,2,32,256]{3,2,1,0:T(8,128)} async-done(((f32[64,2,32,256]{3,2,1,0:T(8,128)}), f32[64,2,32,256]{3,2,1,0:T(8,128)}, u32[]{:S(2)}, u32[]{:S(2)}) %all-to-all-start.5) | async-done | bytes 4194336 | tf_op jit(solution)/shard_map/all_to_all | solution.py:97
  396.4 5.5 %copy.69 = f32[16,8,32,256]{3,1,2,0:T(8,128)S(1)} copy(f32[16,8,32,256]{3,2,1,0:T(8,128)} %bitcast.23) | data formatting | bytes 8388608
  401.9 1.5 convolution_negate_fusion
  403.4 0.8 copy.67
  (13 shorter events, 0.2 us)
Async XLA Ops:
  0.0 35.2 %copy-start = (bf16[8,32,256]{2,1,0:T(8,128)(2,1)S(1)}, bf16[8,32,256]{2,1,0:T(8,128)(2,1)}, u32[]{:S(2)}) copy-start(bf16[8,32,256]{2,1,0:T(8,128)(2,1)} %param.4) | copy-start | bytes 393220
  37.5 5.6 %copy-start.2 = (s32[8,2,1]{0,2,1:T(1,128)S(1)}, s32[8,2,1]{0,2,1:T(1,128)}, u32[]{:S(2)}) copy-start(s32[8,2,1]{0,2,1:T(1,128)} %param.6) | copy-start | bytes 196
  37.5 104.6 %copy-start.1 = (f32[32,256]{1,0:T(8,128)S(1)}, f32[32,256]{1,0:T(8,128)}, u32[]{:S(2)}) copy-start(f32[32,256]{1,0:T(8,128)} %param.5) | copy-start | bytes 98308
  37.5 104.6 %all-to-all-start.2 = ((bf16[64,2,32,256]{3,2,1,0:T(8,128)(2,1)}), bf16[64,2,32,256]{3,2,1,0:T(8,128)(2,1)S(1)}, u32[]{:S(2)}, u32[]{:S(2)}) async-start(bf16[64,2,32,256]{3,2,1,0:T(8,128)(2,1)} %select_select_fusion), calls=%async_computation.2 | async-start | bytes 4194304 | tf_op jit(solution)/shard_map/all_to_all | solution.py:80
  142.8 11.8 %all-to-all-start.1 = ((f32[8,32,256]{2,1,0:T(8,128)}), f32[8,32,256]{2,1,0:T(8,128)S(1)}, u32[]{:S(2)}, u32[]{:S(2)}) async-start(f32[8,32,256]{2,1,0:T(8,128)} %broadcast_in_dim.70), calls=%async_computation.1 | async-start | bytes 524288 | tf_op jit(solution)/shard_map/all_to_all | solution.py:10
  154.6 10.9 %all-to-all-start.3 = ((f32[8,32,256]{2,1,0:T(8,128)}), f32[8,32,256]{2,1,0:T(8,128)S(1)}, u32[]{:S(2)}, u32[]{:S(2)}) async-start(f32[8,32,256]{2,1,0:T(8,128)} %multiply_bitcast_fusion), calls=%async_computation.3 | async-start | bytes 524288 | tf_op jit(solution)/shard_map/all_to_all | solution.py:36
  200.8 195.7 %all-to-all-start.5 = ((f32[64,2,32,256]{3,2,1,0:T(8,128)}), f32[64,2,32,256]{3,2,1,0:T(8,128)}, u32[]{:S(2)}, u32[]{:S(2)}) async-start(f32[64,2,32,256]{3,2,1,0:T(8,128)} %bitcast.53), calls=%async_computation.5 | async-start | bytes 8388608 | tf_op jit(solution)/shard_map/all_to_all | solution.py:97
where the time goes:
time: 405 us; the launch traced here: 404 us
  waiting for transfers between devices  300 us (74%)
  blocking collectives  42.3 us (10%)
  matrix products  21.3 us (5%)
  starting transfers between devices  19.5 us (5%)
  local copies, waits for them, and re-layouts  17.2 us (4%)
    all_to_all x1, waiting for transfers between devices, on_device(): lax.all_to_all(outgoing, 'orb', split_axis=0, concat_axis=0, tiled=True)  188 us
    all_to_all x1, waiting for transfers between devices, on_device(): lax.all_to_all(served, 'orb', split_axis=0, concat_axis=0, tiled=True)  98.6 us
    all_to_all x1, blocking collectives, on_device(): lax.all_to_all(wanted, 'orb', split_axis=0, concat_axis=0, tiled=True)  32.3 us
    dot_general x12, matrix products, product(): return jnp.einsum(form, left, right, precision=lax.Precision.HIGHEST)  19.8 us
    all_to_all x1, blocking collectives, group_potential(): lax.all_to_all(spread, 'fft', split_axis=1, concat_axis=0, tiled=True)  9.91 us
  transfers between devices with their start and end apart: 4, of which 4 were waited for; matrix products, arithmetic and copies ran while one was open for 1% of the time, Pallas kernels for 0%

commit v1 on v0

--- a/solution.py
+++ b/solution.py
@@ -33,7 +33,15 @@
 
 
 def group_potential(density, kernel):
-    grouped = lax.all_to_all(density, "fft", split_axis=0, concat_axis=1, tiled=True)
+    grouped = jnp.concatenate(
+        lax.all_to_all(
+            jnp.stack(jnp.split(density, lax.psum(1, axis_name="fft"), axis=0)),
+            axis_name="fft",
+            split_axis=0,
+            concat_axis=0,
+        ),
+        axis=1,
+    )
     whole = gathered_copies(kernel, "fft", 0)
     full_x = grouped.shape[1]
     width_y = grouped.shape[2]

time: 405 us -> 405 us (level)
  no operation moved by 1% of the time
where the time goes in v1:
time: 405 us; the launch traced here: 404 us
  waiting for transfers between devices  300 us (74%)
  blocking collectives  42.3 us (10%)
  matrix products  21.3 us (5%)
  starting transfers between devices  19.5 us (5%)
  local copies, waits for them, and re-layouts  17.2 us (4%)
    all_to_all x1, waiting for transfers between devices, on_device(): lax.all_to_all(outgoing, 'orb', split_axis=0, concat_axis=0, tiled=True)  188 us
    all_to_all x1, waiting for transfers between devices, on_device(): lax.all_to_all(served, 'orb', split_axis=0, concat_axis=0, tiled=True)  98.6 us
    all_to_all x1, blocking collectives, on_device(): lax.all_to_all(wanted, 'orb', split_axis=0, concat_axis=0, tiled=True)  32.3 us
    dot_general x12, matrix products, product(): return jnp.einsum(form, left, right, precision=lax.Precision.HIGHEST)  19.8 us
    all_to_all x1, blocking collectives, group_potential(): lax.all_to_all(spread, 'fft', split_axis=1, concat_axis=0, tiled=True)  9.91 us
  transfers between devices with their start and end apart: 4, of which 4 were waited for; matrix products, arithmetic and copies ran while one was open for 1% of the time, Pallas kernels for 0%

profile of v1, /device:TPU:8, one launch (start us, length us, event | category | flops | bytes accessed | tf_op | source)
XLA Modules:
  0.0 404.2 jit_solution(12548411028635859213)
XLA Ops:
  0.0 0.0 copy-start
  0.0 0.8 copy.55
  0.8 0.1 broadcast_in_dim.66
  0.9 0.8 copy.54
  1.6 0.1 reshape.203
  1.7 0.1 fusion.30
  1.8 0.2 select_reduce_fusion.1
  2.0 0.1 select_reduce_fusion
  2.1 0.1 all_to_all.27
  2.3 32.3 %all_to_all.41 = s32[64,1,2]{2,1,0:T(1,128)S(1)} all-to-all(s32[64,1,2]{2,1,0:T(1,128)S(1)} %bitcast.62), channel_id=1, replica_groups=mesh['orb'=64,'fft'=8] {'orb'}, dimensions={0} | all-to-all | bytes 1024 | tf_op jit(solution)/shard_map/all_to_all | solution.py:82
  34.6 0.1 copy.61
  34.7 0.1 copy.62
  34.8 0.1 copy.64
  34.9 0.1 copy.65
  35.0 0.1 min.18
  35.2 0.0 copy-done
  35.2 0.7 gather_fusion
  35.9 1.6 select_select_fusion
  37.5 0.0 copy-start.2
  37.5 0.0 copy-start.1
  37.5 5.5 %all-to-all-start.2 = ((bf16[64,2,32,256]{3,2,1,0:T(8,128)(2,1)}), bf16[64,2,32,256]{3,2,1,0:T(8,128)(2,1)S(1)}, u32[]{:S(2)}, u32[]{:S(2)}) async-start(bf16[64,2,32,256]{3,2,1,0:T(8,128)(2,1)} %select_select_fusion), calls=%async_computation.2 | async-start | bytes 4194304 | tf_op jit(solution)/shard_map/all_to_all | solution.py:88
  43.0 0.1 reduce_sum.15
  43.1 0.0 copy-done.2
  43.1 0.1 copy.57
  43.2 0.1 mul.162
  43.3 0.1 copy.59
  43.4 0.1 copy.60
  43.5 98.6 %all-to-all-done.2 = bf16[64,2,32,256]{3,2,1,0:T(8,128)(2,1)S(1)} async-done(((bf16[64,2,32,256]{3,2,1,0:T(8,128)(2,1)}), bf16[64,2,32,256]{3,2,1,0:T(8,128)(2,1)S(1)}, u32[]{:S(2)}, u32[]{:S(2)}) %all-to-all-start.2) | async-done | bytes 2097184 | tf_op jit(solution)/shard_map/all_to_all | solution.py:88
  142.1 0.0 copy-done.1
  142.1 0.7 broadcast_in_dim.70
  142.8 4.3 %all-to-all-start.1 = ((f32[8,32,256]{2,1,0:T(8,128)}), f32[8,32,256]{2,1,0:T(8,128)S(1)}, u32[]{:S(2)}, u32[]{:S(2)}) async-start(f32[8,32,256]{2,1,0:T(8,128)} %broadcast_in_dim.70), calls=%async_computation.1 | async-start | bytes 524288 | tf_op jit(solution)/shard_map/all_to_all | solution.py:10
  147.1 0.6 gather_fusion.1
  147.7 0.1 select_convert_fusion
  147.8 0.7 slice_multiply_fusion.1
  148.6 6.1 %all-to-all-done.1 = f32[8,32,256]{2,1,0:T(8,128)S(1)} async-done(((f32[8,32,256]{2,1,0:T(8,128)}), f32[8,32,256]{2,1,0:T(8,128)S(1)}, u32[]{:S(2)}, u32[]{:S(2)}) %all-to-all-start.1) | async-done | bytes 262176 | tf_op jit(solution)/shard_map/all_to_all | solution.py:10
  154.6 3.6 all-to-all-start.3
  158.2 0.1 copy.58
  158.4 7.1 %all-to-all-done.3 = f32[8,1,32,256]{3,2,1,0:T(8,128)S(1)} async-done(((f32[8,1,32,256]{3,2,1,0:T(8,128)}), f32[8,1,32,256]{3,2,1,0:T(8,128)S(1)}, u32[]{:S(2)}, u32[]{:S(2)}) %all-to-all-start.3) | async-done | bytes 262176 | tf_op jit(solution)/shard_map/all_to_all | solution.py:37
  165.5 1.4 convolution_negate_fusion.1
  166.9 1.3 fusion.21
  168.2 1.8 fusion.19
  170.0 1.8 fusion.15
  171.8 1.8 fusion.3
  173.5 1.8 fusion.24
  175.3 1.8 fusion.17
  177.1 1.8 fusion.2
  178.9 1.8 convolution_subtract_fusion.1
  180.6 2.0 convolution_add_fusion
  182.6 1.3 fusion.13
  184.0 1.4 fusion.1
  185.4 0.3 copy.66
  185.6 9.9 %all_to_all.42 = f32[1,256,256]{2,0,1:T(1,128)S(1)} all-to-all(f32[1,256,256]{2,0,1:T(1,128)S(1)} %copy.66), channel_id=1, replica_groups=mesh['orb'=64,'fft'=8] {'fft'}, dimensions={1} | all-to-all | bytes 524288 | tf_op jit(solution)/shard_map/all_to_all | solution.py:61
  195.6 0.1 slice_multiply_fusion
  195.7 2.5 broadcast_in_dim.69
  198.2 2.6 scatter_fusion
  200.8 6.1 %all-to-all-start.5 = ((f32[64,2,32,256]{3,2,1,0:T(8,128)}), f32[64,2,32,256]{3,2,1,0:T(8,128)}, u32[]{:S(2)}, u32[]{:S(2)}) async-start(f32[64,2,32,256]{3,2,1,0:T(8,128)} %bitcast.51), calls=%async_computation.5 | async-start | bytes 8388608 | tf_op jit(solution)/shard_map/all_to_all | solution.py:105
  206.9 0.5 broadcast.212
  207.4 0.7 reduce.3
  208.1 0.1 eq.50
  208.3 188.2 %all-to-all-done.5 = f32[64,2,32,256]{3,2,1,0:T(8,128)} async-done(((f32[64,2,32,256]{3,2,1,0:T(8,128)}), f32[64,2,32,256]{3,2,1,0:T(8,128)}, u32[]{:S(2)}, u32[]{:S(2)}) %all-to-all-start.5) | async-done | bytes 4194336 | tf_op jit(solution)/shard_map/all_to_all | solution.py:105
  396.4 5.5 %copy.69 = f32[16,8,32,256]{3,1,2,0:T(8,128)S(1)} copy(f32[16,8,32,256]{3,2,1,0:T(8,128)} %bitcast.22) | data formatting | bytes 8388608
  401.9 1.5 convolution_negate_fusion
  403.4 0.8 copy.67
  (13 shorter events, 0.2 us)
Async XLA Ops:
  0.0 35.2 %copy-start = (bf16[8,32,256]{2,1,0:T(8,128)(2,1)S(1)}, bf16[8,32,256]{2,1,0:T(8,128)(2,1)}, u32[]{:S(2)}) copy-start(bf16[8,32,256]{2,1,0:T(8,128)(2,1)} %param.4) | copy-start | bytes 393220
  37.5 5.6 %copy-start.2 = (s32[8,2,1]{0,2,1:T(1,128)S(1)}, s32[8,2,1]{0,2,1:T(1,128)}, u32[]{:S(2)}) copy-start(s32[8,2,1]{0,2,1:T(1,128)} %param.6) | copy-start | bytes 196
  37.5 104.6 %copy-start.1 = (f32[32,256]{1,0:T(8,128)S(1)}, f32[32,256]{1,0:T(8,128)}, u32[]{:S(2)}) copy-start(f32[32,256]{1,0:T(8,128)} %param.5) | copy-start | bytes 98308
  37.5 104.6 %all-to-all-start.2 = ((bf16[64,2,32,256]{3,2,1,0:T(8,128)(2,1)}), bf16[64,2,32,256]{3,2,1,0:T(8,128)(2,1)S(1)}, u32[]{:S(2)}, u32[]{:S(2)}) async-start(bf16[64,2,32,256]{3,2,1,0:T(8,128)(2,1)} %select_select_fusion), calls=%async_computation.2 | async-start | bytes 4194304 | tf_op jit(solution)/shard_map/all_to_all | solution.py:88
  142.8 11.8 %all-to-all-start.1 = ((f32[8,32,256]{2,1,0:T(8,128)}), f32[8,32,256]{2,1,0:T(8,128)S(1)}, u32[]{:S(2)}, u32[]{:S(2)}) async-start(f32[8,32,256]{2,1,0:T(8,128)} %broadcast_in_dim.70), calls=%async_computation.1 | async-start | bytes 524288 | tf_op jit(solution)/shard_map/all_to_all | solution.py:10
  154.6 10.9 %all-to-all-start.3 = ((f32[8,1,32,256]{3,2,1,0:T(8,128)}), f32[8,1,32,256]{3,2,1,0:T(8,128)S(1)}, u32[]{:S(2)}, u32[]{:S(2)}) async-start(f32[8,1,32,256]{3,2,1,0:T(8,128)} %slice_multiply_fusion.1), calls=%async_computation.3 | async-start | bytes 524288 | tf_op jit(solution)/shard_map/all_to_all | solution.py:37
  200.8 195.7 %all-to-all-start.5 = ((f32[64,2,32,256]{3,2,1,0:T(8,128)}), f32[64,2,32,256]{3,2,1,0:T(8,128)}, u32[]{:S(2)}, u32[]{:S(2)}) async-start(f32[64,2,32,256]{3,2,1,0:T(8,128)} %bitcast.51), calls=%async_computation.5 | async-start | bytes 8388608 | tf_op jit(solution)/shard_map/all_to_all | solution.py:105
